TPU v7x, 16 devices: a 4x2x1 block of a 4x4x8 slice. The times are simulated.
16 devices in a mesh: data: 2 (over y, z), time: 8 (over x, core).
Axes of the slice: x: 4, y: 2, z: 1, core: 2. Of those that a mesh axis runs over, the one named last changes fastest.
The devices are a block of a 4x4x8 slice.
Arguments:
- x_init: float32 [16, 256, 16], P('data'), parts along dimension 0
- w_in: bfloat16 [16, 384], replicated
- w_out: bfloat16 [384, 16], replicated
- mod_scale: bfloat16 [32, 384], P('time')
- mod_shift: bfloat16 [32, 384], P('time')
- step_size: float32 [32], P('time')
- noise_inc: float32 [32, 16, 256, 16], P('time', 'data'), parts along dimension 1
Outputs:
- output: float32 [32, 16, 256, 16], P('time', 'data'), parts along dimension 1
There are 2 independent parts. A program takes and returns all parts, laid end to end along the dimension named above; an argument that names none is the same for every part.
All inputs are finite; a program needn't handle non-finite values.
Results may differ from a plain program's by a relative error of at most 0.001.
Values are sent between devices in bfloat16 or wider.
A program may use at most 768 MiB of HBM per device.

v0:
```python
import functools
import math

import jax
import jax.numpy as jnp
from jax import lax
from jax.experimental import pallas as pl
from jax.experimental.pallas import tpu as pltpu
from jax.sharding import PartitionSpec as P

SWEEPS = 8
LANES = 128
F32 = jnp.float32
BF16 = jnp.bfloat16
MESH = pl.DeviceIdType.MESH
GELU_1 = 2.0 * math.sqrt(2.0 / math.pi)
GELU_3 = 4.0 * 0.044715 * GELU_1
CONST_ROW = 64


def gelu_of_half(half):
    inner = half * (half * half * GELU_3 + GELU_1)
    return half + half * jnp.tanh(inner)


def sampler_kernel(n_time, x_ref, w_in_ref, w_out_ref, scale_ref, shift_ref, step_ref, noise_ref, out_ref,
                   x_buf, w_in_t, mod_own, step_own, mod_all, step_all, mod_t, mul_buf, add_buf, pre_init,
                   versions, act_buf, act_late, noise_all, out_stage,
                   x_sem, mod_send, mod_recv, step_send, step_recv, noise_send, noise_recv, out_send, out_recv):
    me = lax.axis_index("time")
    local_steps = scale_ref.shape[0]
    n_steps = n_time * local_steps
    hidden = w_in_ref.shape[1]
    tokens = x_buf.shape[1]
    copies = tokens // LANES

    barrier = pltpu.get_barrier_semaphore()
    for away in range(1, n_time):
        pl.semaphore_signal(barrier, inc=1, device_id={"time": lax.rem(me + away, n_time)}, device_id_type=MESH)

    x_copy = pltpu.make_async_copy(x_ref.at[me], x_buf, x_sem)
    x_copy.start()
    own_noise = pltpu.make_async_copy(noise_ref.at[:, me], noise_all.at[pl.ds(me * local_steps, local_steps)], noise_recv.at[me])
    own_noise.start()
    mod_own[0:local_steps, :] = scale_ref[...]
    mod_own[local_steps:2 * local_steps, :] = shift_ref[...]
    for i in range(local_steps):
        step_own[i:i + 1, :] = jnp.full((1, LANES), step_ref[i], F32)
    mod_all[me] = mod_own[...]
    step_all[me] = step_own[...]
    w_in_t[...] = w_in_ref[...].astype(F32).T.astype(BF16)

    pl.semaphore_wait(barrier, n_time - 1)

    sends = []

    def send(src, dst, send_sem, recv_sem, target):
        copy = pltpu.make_async_remote_copy(src_ref=src, dst_ref=dst, send_sem=send_sem, recv_sem=recv_sem,
                                            device_id={"time": target}, device_id_type=MESH)
        copy.start()
        return copy

    for away in range(1, n_time):
        target = lax.rem(me + away, n_time)
        sends.append(send(mod_own, mod_all.at[me], mod_send.at[away], mod_recv.at[away], target))
        sends.append(send(step_own, step_all.at[me], step_send.at[away], step_recv.at[away], target))
    for away in range(1, n_time):
        target = lax.rem(me + away, n_time)
        sends.append(send(noise_ref.at[:, target], noise_all.at[pl.ds(me * local_steps, local_steps)],
                          noise_send.at[away], noise_recv.at[me], target))

    x_copy.wait()
    x0 = x_buf[...]
    for s in range(SWEEPS + 1):
        versions[s] = x0
    pre_init[...] = jnp.dot(w_in_t[...], x0.astype(BF16), preferred_element_type=F32)

    for away in range(1, n_time):
        source = lax.rem(me + n_time - away, n_time)
        pltpu.make_async_copy(mod_own, mod_all.at[source], mod_recv.at[away]).wait()
        pltpu.make_async_copy(step_own, step_all.at[source], step_recv.at[away]).wait()

    rows = mod_all[...].astype(F32).reshape(n_time * 2 * local_steps, hidden)
    pad = (lax.broadcasted_iota(jnp.int32, (LANES - CONST_ROW, hidden), 0) == 0).astype(F32)
    mod_t[...] = jnp.concatenate([rows, pad], axis=0).T.astype(BF16)

    def column_of(block, i):
        block = block + i // local_steps
        return block * 2 * local_steps + i % local_steps

    def prepare(block, steps):
        row = lax.broadcasted_iota(jnp.int32, (LANES, LANES), 0)
        picks = []
        for i in steps:
            at = column_of(block, i)
            picks.append(jnp.where((row == at) | (row == CONST_ROW), 0.5, 0.0).astype(BF16))
            picks.append(jnp.where(row == at + local_steps, 0.5, 0.0).astype(BF16))
        both = jnp.dot(mod_t[...], jnp.concatenate(picks, axis=1), preferred_element_type=F32)
        for k, i in enumerate(steps):
            mul_buf[i % local_steps] = both[:, 2 * k * LANES:(2 * k + 1) * LANES]
            add_buf[i % local_steps] = both[:, (2 * k + 1) * LANES:(2 * k + 2) * LANES]

    def wide(row):
        return jnp.concatenate([row] * copies, axis=1)

    def activate(pre, slot, dst, index):
        half = pre * wide(mul_buf[slot]) + wide(add_buf[slot])
        dst[index] = gelu_of_half(half).astype(BF16)

    def first_product(s):
        return jnp.dot(w_in_t[...], versions[s].astype(BF16), preferred_element_type=F32)

    def update(block, i, s, act, base=None):
        at = block * local_steps + i
        drift = jnp.dot(w_out_ref[...], act, preferred_element_type=F32)
        step = wide(step_all[block + i // local_steps, pl.ds(i % local_steps, 1), :])
        versions[s + 1] = versions[s + 1 if base is None else base] + (drift * step + noise_all[at])

    def run_block(block, first, last, static_block=None, late=None, keep_late=True):
        for i in range(first, last):
            if static_block is None:
                low, high = 0, SWEEPS - 1
            else:
                j = static_block * local_steps + i
                low, high = max(0, SWEEPS - (n_steps - 1 - j)), min(j, SWEEPS - 1)
            slot = i % local_steps
            out_stage[block * local_steps + i] = versions[min(high + 1, SWEEPS) if static_block is None or j >= SWEEPS else j]
            if low > high:
                continue
            if i % 2 == 0:
                steps = (i + 1, i + 2)
                if static_block is not None:
                    steps = tuple(k for k in steps if static_block * local_steps + k < n_steps - 1)
                if steps:
                    prepare(block, steps)
            if late is not None:
                update(*late, act_late[...])
                late = None
            order = ([0] if low == 0 else []) + list(range(high, max(low, 1) - 1, -1))
            pre = pre_init[...] if order[0] == 0 else first_product(order[0])
            waiting = []
            for k, s in enumerate(order):
                following = first_product(order[k + 1]) if k + 1 < len(order) else None
                is_late = keep_late and i == last - 1 and k == len(order) - 1 and s != 0
                if is_late:
                    activate(pre, slot, act_late, ...)
                    late = (block, i, s)
                else:
                    activate(pre, slot, act_buf, (i % 2) * SWEEPS + s)
                pre = following
                waiting.append(s)
                ready = [w for w in waiting[:-1] if w != 0]
                for w in ready:
                    fresh = static_block is not None and w == j
                    update(block, i, w, act_buf[(i % 2) * SWEEPS + w], w if fresh else None)
                    waiting.remove(w)
            for w in sorted(waiting, reverse=True):
                if late is not None and w == late[2]:
                    continue
                fresh = static_block is not None and w == j
                update(block, i, w, act_buf[(i % 2) * SWEEPS + w], w if fresh else None)
        return late

    def wait_noise(block):
        dst = noise_all.at[pl.ds(block * local_steps, local_steps)]
        pltpu.make_async_copy(noise_ref.at[:, me], dst, noise_recv.at[block]).wait()

    def send_block(block):
        src = out_stage.at[pl.ds(block * local_steps, local_steps)]

        @pl.when(block != me)
        def _():
            send(src, out_ref.at[:, me], out_send.at[block], out_recv.at[me], block)

        @pl.when(block == me)
        def _():
            out_ref[:, me] = src[...]

    full_from = -(-(SWEEPS - 1) // local_steps)
    full_to = (n_steps - SWEEPS) // local_steps

    prepare(0, (0,))
    late = None
    for block in range(full_from):
        wait_noise(block)
        late = run_block(block, 0, local_steps, block, late)
        if block > 0:
            send_block(block - 1)

    def body(block, carry):
        wait_noise(block)
        send_block(block - 1)
        run_block(block, 0, local_steps, None, (block - 1, local_steps - 1, 1))
        return carry

    lax.fori_loop(full_from, full_to, body, 0)
    late = (full_to - 1, local_steps - 1, 1)
    for block in range(full_to, n_time):
        wait_noise(block)
        send_block(block - 1)
        late = run_block(block, 0, local_steps, block, late, keep_late=block < n_time - 1)
    send_block(n_time - 1)

    for copy in sends:
        copy.wait_send()
    for away in range(1, n_time):
        other = lax.rem(me + away, n_time)
        done = pltpu.make_async_remote_copy(src_ref=out_stage.at[pl.ds(other * local_steps, local_steps)], dst_ref=out_ref.at[:, other],
                                            send_sem=out_send.at[other], recv_sem=out_recv.at[other],
                                            device_id={"time": other}, device_id_type=MESH)
        done.wait_send()
        done.wait_recv()


def solution(mesh):
    n_time = mesh.shape["time"]

    def body(x_init, w_in, w_out, mod_scale, mod_shift, step_size, noise_inc):
        local_steps, batch, tokens, channels = noise_inc.shape
        hidden = w_in.shape[1]
        assert batch == n_time and 2 * local_steps * n_time == CONST_ROW
        x_t = jnp.swapaxes(x_init, 1, 2)
        noise_t = jnp.swapaxes(noise_inc, 2, 3)
        n_steps = n_time * local_steps
        vmem = pl.BlockSpec(memory_space=pltpu.VMEM)
        anywhere = pl.BlockSpec(memory_space=pl.ANY)
        dma = pltpu.SemaphoreType.DMA
        out = pl.pallas_call(
            functools.partial(sampler_kernel, n_time),
            out_shape=jax.ShapeDtypeStruct(noise_t.shape, F32),
            in_specs=[anywhere, vmem, vmem, vmem, vmem, pl.BlockSpec(memory_space=pltpu.SMEM), anywhere],
            out_specs=vmem,
            scratch_shapes=[
                pltpu.VMEM((channels, tokens), F32),
                pltpu.VMEM((hidden, channels), BF16),
                pltpu.VMEM((2 * local_steps, hidden), BF16),
                pltpu.VMEM((2 * local_steps, LANES), F32),
                pltpu.VMEM((n_time, 2 * local_steps, hidden), BF16),
                pltpu.VMEM((n_time, 2 * local_steps, LANES), F32),
                pltpu.VMEM((hidden, LANES), BF16),
                pltpu.VMEM((local_steps, hidden, LANES), F32),
                pltpu.VMEM((local_steps, hidden, LANES), F32),
                pltpu.VMEM((hidden, tokens), F32),
                pltpu.VMEM((SWEEPS + 1, channels, tokens), F32),
                pltpu.VMEM((2 * SWEEPS, hidden, tokens), BF16),
                pltpu.VMEM((hidden, tokens), BF16),
                pltpu.VMEM((n_steps, channels, tokens), F32),
                pltpu.VMEM((n_steps, channels, tokens), F32),
                dma, dma((n_time,)), dma((n_time,)), dma((n_time,)), dma((n_time,)),
                dma((n_time,)), dma((n_time,)), dma((n_time,)), dma((n_time,)),
            ],
            compiler_params=pltpu.CompilerParams(collective_id=0, has_side_effects=True),
        )(x_t, w_in, w_out.T, mod_scale, mod_shift, step_size, noise_t)
        return jnp.swapaxes(out, 2, 3)

    return jax.shard_map(
        body,
        mesh=mesh,
        in_specs=(P("data"), P(), P(), P("time"), P("time"), P("time"), P("time", "data")),
        out_specs=P("time", "data"),
        check_vma=False,
    )
```

profile of v0, /device:TPU:119, one launch (start us, length us, event | category | flops | bytes accessed | tf_op | source)
XLA Modules:
  0.0 48.4 jit_solution(5375405742713665941)
XLA Ops:
  0.0 46.5 %shard_map.73 = f32[4,8,16,256]{3,2,1,0:T(8,128)} custom-call(f32[8,16,256]{2,1,0:T(8,128)} %bitcast.6, bf16[16,384]{1,0:T(8,128)(2,1)} %w_in_ref.1, bf16[16,384]{1,0:T(8,128)(2,1)} %bitcast.7, bf16[4,384]{1,0:T(4,128)(2,1)} %scale_ref.1, bf16[4,384]{1,0:T(4,128)(2,1)} %shift_ref.1, f32[4]{0:T(128)} %step_ref.1, f32[4,8,16,256]{3,2,1,0:T(8,128)} %bitcast.5), custom_call_target="tpu_custom_call" | custom-call | tf_op jit(solution)/shard_map/pallas_call | solution.py:228
  46.6 1.9 %copy.9 = f32[4,8,256,16]{2,3,1,0:T(8,128)} copy(f32[4,8,256,16]{2,3,1,0:T(8,128)} %bitcast.4) | data formatting | bytes 1048576
where the time goes:
time: 48.6 us; the launch traced here: 48.4 us
  Pallas kernels  46.5 us (96%)
  local copies, waits for them, and re-layouts  1.87 us (4%)
    pallas_call x1, Pallas kernels, body(): pl.pallas_call(functools.partial(sampler_kernel, n_time), out_shape=jax.S...  46.5 us
    unnamed x1, local copies, waits for them, and re-layouts  1.87 us

commit v1 on v0

--- a/solution.py
+++ b/solution.py
@@ -24,11 +24,13 @@
 
 
 def sampler_kernel(n_time, x_ref, w_in_ref, w_out_ref, scale_ref, shift_ref, step_ref, noise_ref, out_ref,
-                   x_buf, w_in_t, mod_own, step_own, mod_all, step_all, mod_t, mul_buf, add_buf, pre_init,
-                   versions, act_buf, act_late, noise_all, out_stage,
-                   x_sem, mod_send, mod_recv, step_send, step_recv, noise_send, noise_recv, out_send, out_recv):
+                   x_buf, w_in_buf, w_out_buf, scale_buf, shift_buf, step_buf,
+                   w_in_t, mod_own, step_own, mod_all, step_all, mod_t, mul_buf, add_buf, pre_init,
+                   versions, act_buf, act_late, noise_all, out_stage, gathered,
+                   load_sem, mod_send, mod_recv, step_send, step_recv, noise_send, noise_recv, out_send, out_recv):
     me = lax.axis_index("time")
     local_steps = scale_ref.shape[0]
+    partner = me + 1 - 2 * lax.rem(me, 2)
     n_steps = n_time * local_steps
     hidden = w_in_ref.shape[1]
     tokens = x_buf.shape[1]
@@ -38,17 +40,30 @@
     for away in range(1, n_time):
         pl.semaphore_signal(barrier, inc=1, device_id={"time": lax.rem(me + away, n_time)}, device_id_type=MESH)
 
-    x_copy = pltpu.make_async_copy(x_ref.at[me], x_buf, x_sem)
-    x_copy.start()
+    loads = [
+        pltpu.make_async_copy(src, dst, load_sem.at[k])
+        for k, (src, dst) in enumerate([(scale_ref, scale_buf), (shift_ref, shift_buf), (step_ref, step_buf),
+                                        (w_in_ref, w_in_buf), (x_ref.at[me], x_buf), (w_out_ref, w_out_buf)])
+    ]
+    for copy in loads:
+        copy.start()
     own_noise = pltpu.make_async_copy(noise_ref.at[:, me], noise_all.at[pl.ds(me * local_steps, local_steps)], noise_recv.at[me])
     own_noise.start()
-    mod_own[0:local_steps, :] = scale_ref[...]
-    mod_own[local_steps:2 * local_steps, :] = shift_ref[...]
+    for copy in loads:
+        copy.wait()
+    mod_own[0:local_steps, :] = scale_buf[...]
+    mod_own[local_steps:2 * local_steps, :] = shift_buf[...]
     for i in range(local_steps):
-        step_own[i:i + 1, :] = jnp.full((1, LANES), step_ref[i], F32)
+        step_own[i:i + 1, :] = jnp.full((1, LANES), step_buf[i], F32)
     mod_all[me] = mod_own[...]
     step_all[me] = step_own[...]
-    w_in_t[...] = w_in_ref[...].astype(F32).T.astype(BF16)
+    w_in_t[...] = w_in_buf[...].astype(F32).T.astype(BF16)
+
+    x0 = x_buf[...]
+    for s in range(SWEEPS + 1):
+        versions[s] = x0
+    out_stage[0] = x0
+    pre_init[...] = jnp.dot(w_in_t[...], x0.astype(BF16), preferred_element_type=F32)
 
     pl.semaphore_wait(barrier, n_time - 1)
 
@@ -68,12 +83,6 @@
         target = lax.rem(me + away, n_time)
         sends.append(send(noise_ref.at[:, target], noise_all.at[pl.ds(me * local_steps, local_steps)],
                           noise_send.at[away], noise_recv.at[me], target))
-
-    x_copy.wait()
-    x0 = x_buf[...]
-    for s in range(SWEEPS + 1):
-        versions[s] = x0
-    pre_init[...] = jnp.dot(w_in_t[...], x0.astype(BF16), preferred_element_type=F32)
 
     for away in range(1, n_time):
         source = lax.rem(me + n_time - away, n_time)
@@ -105,16 +114,21 @@
 
     def activate(pre, slot, dst, index):
         half = pre * wide(mul_buf[slot]) + wide(add_buf[slot])
-        dst[index] = gelu_of_half(half).astype(BF16)
+        dst[index] = gelu_of_half(half)
 
     def first_product(s):
         return jnp.dot(w_in_t[...], versions[s].astype(BF16), preferred_element_type=F32)
 
     def update(block, i, s, act, base=None):
         at = block * local_steps + i
-        drift = jnp.dot(w_out_ref[...], act, preferred_element_type=F32)
+        done = s == SWEEPS - 1 or base is not None
+        drift = jnp.dot(w_out_buf[...], act.astype(BF16), preferred_element_type=F32)
         step = wide(step_all[block + i // local_steps, pl.ds(i % local_steps, 1), :])
         versions[s + 1] = versions[s + 1 if base is None else base] + (drift * step + noise_all[at])
+        if done:
+            out_stage[at + 1] = versions[s + 1]
+            if isinstance(block, int):
+                send_ready(block, i + 1)
 
     def run_block(block, first, last, static_block=None, late=None, keep_late=True):
         for i in range(first, last):
@@ -124,7 +138,6 @@
                 j = static_block * local_steps + i
                 low, high = max(0, SWEEPS - (n_steps - 1 - j)), min(j, SWEEPS - 1)
             slot = i % local_steps
-            out_stage[block * local_steps + i] = versions[min(high + 1, SWEEPS) if static_block is None or j >= SWEEPS else j]
             if low > high:
                 continue
             if i % 2 == 0:
@@ -165,16 +178,21 @@
         dst = noise_all.at[pl.ds(block * local_steps, local_steps)]
         pltpu.make_async_copy(noise_ref.at[:, me], dst, noise_recv.at[block]).wait()
 
-    def send_block(block):
-        src = out_stage.at[pl.ds(block * local_steps, local_steps)]
-
-        @pl.when(block != me)
-        def _():
-            send(src, out_ref.at[:, me], out_send.at[block], out_recv.at[me], block)
-
-        @pl.when(block == me)
-        def _():
-            out_ref[:, me] = src[...]
+    def send_steps(block, first, count):
+        own = block == me
+        send(out_stage.at[pl.ds(block * local_steps + first, count)],
+             gathered.at[pl.ds(first, count), jnp.where(own, n_time, me)],
+             out_send.at[block], out_recv.at[jnp.where(own, n_time, me)], jnp.where(own, partner, block))
+
+    def send_ready(block, i):
+        block, i = block + i // local_steps, i % local_steps
+        if block == n_time - 2 and i >= local_steps - 2:
+            if i == local_steps - 2:
+                send_steps(block, 0, i + 1)
+            else:
+                send_steps(block, i, 1)
+        if block == n_time - 1:
+            send_steps(block, i, 1)
 
     full_from = -(-(SWEEPS - 1) // local_steps)
     full_to = (n_steps - SWEEPS) // local_steps
@@ -185,11 +203,11 @@
         wait_noise(block)
         late = run_block(block, 0, local_steps, block, late)
         if block > 0:
-            send_block(block - 1)
+            send_steps(block - 1, 0, local_steps)
 
     def body(block, carry):
         wait_noise(block)
-        send_block(block - 1)
+        send_steps(block - 1, 0, local_steps)
         run_block(block, 0, local_steps, None, (block - 1, local_steps - 1, 1))
         return carry
 
@@ -197,19 +215,24 @@
     late = (full_to - 1, local_steps - 1, 1)
     for block in range(full_to, n_time):
         wait_noise(block)
-        send_block(block - 1)
+        if block == full_to:
+            send_steps(block - 1, 0, local_steps)
         late = run_block(block, 0, local_steps, block, late, keep_late=block < n_time - 1)
-    send_block(n_time - 1)
 
     for copy in sends:
         copy.wait_send()
-    for away in range(1, n_time):
+    for away in range(n_time):
         other = lax.rem(me + away, n_time)
-        done = pltpu.make_async_remote_copy(src_ref=out_stage.at[pl.ds(other * local_steps, local_steps)], dst_ref=out_ref.at[:, other],
-                                            send_sem=out_send.at[other], recv_sem=out_recv.at[other],
-                                            device_id={"time": other}, device_id_type=MESH)
+        slot = n_time if away == 0 else other
+        done = pltpu.make_async_remote_copy(src_ref=out_stage.at[pl.ds(other * local_steps, local_steps)], dst_ref=gathered.at[:, slot],
+                                            send_sem=out_send.at[other], recv_sem=out_recv.at[slot],
+                                            device_id={"time": partner}, device_id_type=MESH)
         done.wait_send()
         done.wait_recv()
+        if away == 0:
+            out_ref[:, me] = out_stage[pl.ds(me * local_steps, local_steps)]
+        else:
+            out_ref[:, other] = gathered[:, other]
 
 
 def solution(mesh):
@@ -227,11 +250,16 @@
         dma = pltpu.SemaphoreType.DMA
         out = pl.pallas_call(
             functools.partial(sampler_kernel, n_time),
-            out_shape=jax.ShapeDtypeStruct(noise_t.shape, F32),
-            in_specs=[anywhere, vmem, vmem, vmem, vmem, pl.BlockSpec(memory_space=pltpu.SMEM), anywhere],
+            out_shape=pltpu.VMEM(noise_t.shape, F32),
+            in_specs=[anywhere] * 7,
             out_specs=vmem,
             scratch_shapes=[
                 pltpu.VMEM((channels, tokens), F32),
+                pltpu.VMEM((channels, hidden), BF16),
+                pltpu.VMEM((channels, hidden), BF16),
+                pltpu.VMEM((local_steps, hidden), BF16),
+                pltpu.VMEM((local_steps, hidden), BF16),
+                pltpu.SMEM((local_steps,), F32),
                 pltpu.VMEM((hidden, channels), BF16),
                 pltpu.VMEM((2 * local_steps, hidden), BF16),
                 pltpu.VMEM((2 * local_steps, LANES), F32),
@@ -242,12 +270,13 @@
                 pltpu.VMEM((local_steps, hidden, LANES), F32),
                 pltpu.VMEM((hidden, tokens), F32),
                 pltpu.VMEM((SWEEPS + 1, channels, tokens), F32),
-                pltpu.VMEM((2 * SWEEPS, hidden, tokens), BF16),
-                pltpu.VMEM((hidden, tokens), BF16),
+                pltpu.VMEM((2 * SWEEPS, hidden, tokens), F32),
+                pltpu.VMEM((hidden, tokens), F32),
                 pltpu.VMEM((n_steps, channels, tokens), F32),
                 pltpu.VMEM((n_steps, channels, tokens), F32),
-                dma, dma((n_time,)), dma((n_time,)), dma((n_time,)), dma((n_time,)),
-                dma((n_time,)), dma((n_time,)), dma((n_time,)), dma((n_time,)),
+                pltpu.VMEM((local_steps, n_time + 1, channels, tokens), F32),
+                dma((6,)), dma((n_time,)), dma((n_time,)), dma((n_time,)), dma((n_time,)),
+                dma((n_time,)), dma((n_time,)), dma((n_time,)), dma((n_time + 1,)),
             ],
             compiler_params=pltpu.CompilerParams(collective_id=0, has_side_effects=True),
         )(x_t, w_in, w_out.T, mod_scale, mod_shift, step_size, noise_t)

time: 48.6 us -> 43 us (0.88)
  Pallas kernels: 46.5 us -> 42.1 us
  local copies, waits for them, and re-layouts: 1.87 us -> 0.8 us
    pallas_call x1, Pallas kernels: 46.5 us -> 42.1 us  [body(): pl.pallas_call(functools.partial(sampler_kernel, n_time), out_shape=pltpu...]
    unnamed x1, local copies, waits for them, and re-layouts: 1.87 us -> 0.8 us
where the time goes in v1:
time: 43 us; the launch traced here: 42.9 us
  Pallas kernels  42.1 us (98%)
  local copies, waits for them, and re-layouts  0.8 us (2%)
    pallas_call x1, Pallas kernels, body(): pl.pallas_call(functools.partial(sampler_kernel, n_time), out_shape=pltpu...  42.1 us

profile of v1, /device:TPU:119, one launch (start us, length us, event | category | flops | bytes accessed | tf_op | source)
XLA Modules:
  0.0 42.9 jit_solution(4587580554323512322)
XLA Ops:
  0.0 42.1 %shard_map.73 = f32[4,8,16,256]{3,2,1,0:T(8,128)S(1)} custom-call(f32[8,16,256]{2,1,0:T(8,128)} %bitcast.6, bf16[16,384]{1,0:T(8,128)(2,1)} %w_in_ref.1, bf16[16,384]{1,0:T(8,128)(2,1)} %bitcast.7, bf16[4,384]{1,0:T(4,128)(2,1)} %scale_ref.1, bf16[4,384]{1,0:T(4,128)(2,1)} %shift_ref.1, f32[4]{0:T(128)} %step_ref.1, f32[4,8,16,256]{3,2,1,0:T(8,128)} %bitcast.5), custom_call_target="tpu_custom_call" | custom-call | tf_op jit(solution)/shard_map/pallas_call | solution.py:251
  42.1 0.8 %copy.9 = f32[4,8,256,16]{2,3,1,0:T(8,128)} copy(f32[4,8,256,16]{2,3,1,0:T(8,128)S(1)} %bitcast.4) | data formatting | bytes 1048576

commit v2 on v1

v2 whole, which is shorter than its diff:
```python
import functools
import math

import jax
import jax.numpy as jnp
from jax import lax
from jax.experimental import pallas as pl
from jax.experimental.pallas import tpu as pltpu
from jax.sharding import PartitionSpec as P

SWEEPS = 8
UPWARD = 6
LANES = 128
F32 = jnp.float32
BF16 = jnp.bfloat16
MESH = pl.DeviceIdType.MESH
GELU_1 = 2.0 * math.sqrt(2.0 / math.pi)
GELU_3 = 4.0 * 0.044715 * GELU_1


def gelu_of_half(half):
    inner = half * (half * half * GELU_3 + GELU_1)
    return half + half * jnp.tanh(inner)


def sampler_kernel(n_time, x_ref, w_in_ref, w_out_ref, scale_ref, shift_ref, step_ref, noise_ref, out_ref,
                   x_buf, w_in_buf, w_out_buf, scale_buf, shift_buf, step_buf, noise_buf,
                   w_in_t, mod_own, step_own, mod_all, step_all, mul_all, add_all, pre_init, first_drift,
                   versions, act_buf, act_late, pre_late, act_init, noise_all, out_stage, gathered,
                   load_sem, mod_send, mod_recv, step_send, step_recv, noise_send, noise_recv, out_send, out_recv):
    me = lax.axis_index("time")
    local_steps = scale_ref.shape[0]
    partner = me + 1 - 2 * lax.rem(me, 2)
    n_steps = n_time * local_steps
    hidden = w_in_ref.shape[1]
    tokens = x_buf.shape[1]
    copies = tokens // LANES

    barrier = pltpu.get_barrier_semaphore()
    for away in range(1, n_time):
        pl.semaphore_signal(barrier, inc=1, device_id={"time": lax.rem(me + away, n_time)}, device_id_type=MESH)

    loads = [
        pltpu.make_async_copy(src, dst, load_sem.at[k])
        for k, (src, dst) in enumerate([(scale_ref, scale_buf), (shift_ref, shift_buf), (step_ref, step_buf),
                                        (w_in_ref, w_in_buf), (x_ref.at[me], x_buf), (w_out_ref, w_out_buf)])
    ]
    for copy in loads:
        copy.start()
    own_noise = pltpu.make_async_copy(noise_ref.at[:, me], noise_all.at[pl.ds(me * local_steps, local_steps)], noise_recv.at[me])
    own_noise.start()
    noise_load = pltpu.make_async_copy(noise_ref, noise_buf, load_sem.at[len(loads)])
    noise_load.start()
    for copy in loads:
        copy.wait()
    mod_own[0:local_steps, :] = scale_buf[...]
    mod_own[local_steps:2 * local_steps, :] = shift_buf[...]
    for i in range(local_steps):
        step_own[i:i + 1, :] = jnp.full((1, LANES), step_buf[i], F32)
    mod_all[me] = mod_own[...]
    step_all[me] = step_own[...]
    w_in_t[...] = w_in_buf[...].astype(F32).T.astype(BF16)

    x0 = x_buf[...]
    versions[0, 0] = x0
    versions[1, 0] = x0
    out_stage[0] = x0
    pre_init[...] = jnp.dot(w_in_t[...], x0.astype(BF16), preferred_element_type=F32)

    pl.semaphore_wait(barrier, n_time - 1)

    sends = []

    def send(src, dst, send_sem, recv_sem, target):
        copy = pltpu.make_async_remote_copy(src_ref=src, dst_ref=dst, send_sem=send_sem, recv_sem=recv_sem,
                                            device_id={"time": target}, device_id_type=MESH)
        copy.start()
        return copy

    n_chips = n_time // 2
    chip, core = me // 2, lax.rem(me, 2)
    apart = sorted(range(1, n_chips), key=lambda hops: -min(hops, n_chips - hops))
    peers = [2 * lax.rem(chip + hops, n_chips) + c for hops in apart for c in range(2)] + [partner]
    for k, target in enumerate(peers):
        sends.append(send(mod_own, mod_all.at[me], mod_send.at[k], mod_recv.at[me], target))
        sends.append(send(step_own, step_all.at[me], step_send.at[k], step_recv.at[me], target))
    noise_load.wait()

    def noise_copy(k):
        return pltpu.make_async_remote_copy(
            src_ref=noise_buf.at[:, peers[k]], dst_ref=noise_all.at[pl.ds(me * local_steps, local_steps)],
            send_sem=noise_send.at[k], recv_sem=noise_recv.at[me], device_id={"time": peers[k]}, device_id_type=MESH)

    def send_noise():
        for k in range(n_time - 1):
            noise_copy(k).start()

    def wait_mods(source):
        pltpu.make_async_copy(mod_own, mod_all.at[source], mod_recv.at[source]).wait()
        pltpu.make_async_copy(step_own, step_all.at[source], step_recv.at[source]).wait()

    def wide(row):
        return jnp.concatenate([row] * copies, axis=1)

    def columns(rows, ones_row):
        pad = (lax.broadcasted_iota(jnp.int32, (LANES - ones_row, hidden), 0) == 0).astype(F32)
        return jnp.concatenate([rows, pad], axis=0).T.astype(BF16)

    def spread(cols, picked, ones_row):
        row = lax.broadcasted_iota(jnp.int32, (LANES, LANES), 0)
        picks = []
        for at in picked:
            picks.append(jnp.where((row == at) | (row == ones_row), 0.5, 0.0).astype(BF16))
            picks.append(jnp.where(row == at + local_steps, 0.5, 0.0).astype(BF16))
        both = jnp.dot(cols, jnp.concatenate(picks, axis=1), preferred_element_type=F32)
        parts = [both[:, k * LANES:(k + 1) * LANES] for k in range(2 * len(picked))]
        return parts[0::2], parts[1::2]

    def start_rows(sources):
        rows = jnp.concatenate([mod_all[source].astype(F32) for source in sources], axis=0)
        ones_row = rows.shape[0]
        picked = [2 * local_steps * k + i for k in range(len(sources)) for i in range(local_steps)]
        muls, adds = spread(columns(rows, ones_row), picked, ones_row)
        for k in range(len(picked)):
            at = sources[k // local_steps] * local_steps + k % local_steps
            mul_all[at] = muls[k]
            add_all[at] = adds[k]

    def start_tile(sources, k):
        source, i = sources[k // local_steps], k % local_steps
        at = source * local_steps + i
        half = pre_init[...] * wide(mul_all[at]) + wide(add_all[at])
        act_init[k] = gelu_of_half(half)
        drift = jnp.dot(w_out_buf[...], act_init[k].astype(BF16), preferred_element_type=F32)
        first_drift[at] = drift * wide(step_all[source, pl.ds(i, 1), :])

    needed = (n_steps - SWEEPS) // local_steps
    has_own = me < needed
    nearest = jnp.where(has_own, chip, 0)
    order = [nearest] + [jnp.where(k - 1 < nearest, k - 1, k) for k in range(1, needed // 2)]
    one = 2 * nearest + jnp.where(has_own, core, 0)
    other = 2 * nearest + jnp.where(has_own, 1 - core, 1)

    @pl.when(me == 0)
    def _():
        send_noise()

    @pl.when(one != me)
    def _():
        wait_mods(one)

    start_rows([one])
    for k in range(local_steps):
        start_tile([one], k)
    wait_mods(other)
    start_rows([other])
    for k in range(local_steps):
        start_tile([other], k)

    @pl.when(me == 1)
    def _():
        send_noise()

    for chip_at in order[1:-1]:
        pair = [2 * chip_at, 2 * chip_at + 1]
        for source in pair:
            wait_mods(source)
        start_rows(pair)
        for k in range(2 * local_steps):
            start_tile(pair, k)

    @pl.when(me >= 2)
    def _():
        send_noise()

    pair = [2 * order[-1], 2 * order[-1] + 1]
    for source in pair + list(range(needed, n_time)):
        @pl.when((source != me) & (source != one) & (source != other))
        def _(source=source):
            wait_mods(source)
    start_rows(pair)
    start_rows(range(needed, n_time))

    def activate(pre, at, dst, index):
        half = pre * wide(mul_all[at]) + wide(add_all[at])
        dst[index] = gelu_of_half(half)

    def first_product(parity, s, parts=1):
        size = hidden // parts
        latent = versions[parity, s].astype(BF16)
        return jnp.concatenate([jnp.dot(w_in_t[k * size:(k + 1) * size, :], latent, preferred_element_type=F32) for k in range(parts)], axis=0)

    def update(block, i, s, act, base=None):
        at = block * local_steps + i
        done = s == SWEEPS - 1 or base is not None
        drift = jnp.dot(w_out_buf[...], act.astype(BF16), preferred_element_type=F32)
        step = wide(step_all[block + i // local_steps, pl.ds(i % local_steps, 1), :])
        latent = versions[i % 2, s + 1 if base is None else base] + (drift * step + noise_all[at])
        versions[1 - i % 2, s + 1] = latent
        if done:
            out_stage[at + 1] = latent
            if isinstance(block, int):
                send_ready(block, i + 1)

    def run_block(block, static_block=None, late=(), last=False, filler=(), upward=False):
        filler = list(filler)
        block_parts = last or static_block == 0
        late_act = late_pre = None
        if late:
            late_act, late_pre = late

        def finish(tile):
            if tile == "late":
                update(*late_pre, act_late[...])
                return
            i, s = tile
            fresh = static_block is not None and s == static_block * local_steps + i
            update(block, i, s, act_buf[(i % 2) * SWEEPS + s], s if fresh else None)

        def ranges(i):
            if static_block is None:
                return 1, SWEEPS - 1, True
            j = static_block * local_steps + i
            low = SWEEPS - (n_steps - 1 - j)
            return max(1, low), min(j, SWEEPS - 1), low <= 0

        tiles = [(i, s) for i in range(local_steps) for s in range(ranges(i)[1], ranges(i)[0] - 1, -1)]
        if upward:
            tiles.sort()
        begun = {}

        def begin(tile):
            begun[tile] = first_product(tile[0] % 2, tile[1], 2 if block_parts else 1)

        pending = []
        for i in range(local_steps):
            low, high, needs_first = ranges(i)
            mine = [t for t in tiles if t[0] == i]
            if mine:
                begin(mine[0])
            if late_act is not None:
                update(*late_act, act_late[...])
                activate(pre_late[...], late_pre[0] * local_steps + late_pre[1], act_late, ...)
                pending.append("late")
                late_act = None
                if upward:
                    finish(pending.pop())
            for k, tile in enumerate(mine):
                if k + 1 < len(mine):
                    begin(mine[k + 1])
                pre = begun.pop(tile)
                if not last and tile == tiles[-1]:
                    pre_late[...] = pre
                    late_pre_out = (block, i, tile[1])
                    continue
                if not last and tile == tiles[-2]:
                    activate(pre, block * local_steps + i, act_late, ...)
                    late_act_out = (block, i, tile[1])
                else:
                    activate(pre, block * local_steps + i, act_buf, (i % 2) * SWEEPS + tile[1])
                    pending.append(tile)
                while len(pending) > 1:
                    finish(pending.pop(0))
                if filler:
                    filler.pop(0)()
            while pending:
                finish(pending.pop(0))
            if needs_first:
                at = block * local_steps + i
                fresh = static_block is not None and at == 0
                latent = versions[i % 2, 0 if fresh else 1] + (first_drift[at] + noise_all[at])
                versions[1 - i % 2, 1] = latent
                if fresh:
                    out_stage[1] = latent
        for work in filler:
            work()
        if not last:
            return late_act_out, late_pre_out

    def wait_noise(block):
        dst = noise_all.at[pl.ds(block * local_steps, local_steps)]
        pltpu.make_async_copy(noise_ref.at[:, me], dst, noise_recv.at[block]).wait()

    def send_steps(block, first, count):
        own = block == me
        send(out_stage.at[pl.ds(block * local_steps + first, count)],
             gathered.at[pl.ds(first, count), jnp.where(own, n_time, me)],
             out_send.at[block], out_recv.at[jnp.where(own, n_time, me)], jnp.where(own, partner, block))

    def send_ready(block, i):
        block, i = block + i // local_steps, i % local_steps
        if block == n_time - 2 and i >= local_steps - 2:
            if i == local_steps - 2:
                send_steps(block, 0, i + 1)
            else:
                send_steps(block, i, 1)
        if block == n_time - 1:
            send_steps(block, i, 1)

    full_from = -(-(SWEEPS - 1) // local_steps)
    full_to = (n_steps - SWEEPS) // local_steps

    late = ()
    for block in range(full_from):
        wait_noise(block)
        if block > 0:
            send_steps(block - 1, 0, local_steps)
        filler = [functools.partial(start_tile, pair, k) for k in range(2 * local_steps)] if block == 0 else ()
        late = run_block(block, block, late, filler=filler)

    def late_of(block):
        return (block, local_steps - 1, 2), (block, local_steps - 1, 1)

    def body(block, carry):
        wait_noise(block)
        send_steps(block - 1, 0, local_steps)
        run_block(block, None, late_of(block - 1))
        return carry

    lax.fori_loop(full_from, full_to, body, 0)
    late = late_of(full_to - 1)
    for block in range(full_to, n_time):
        wait_noise(block)
        if block == full_to:
            send_steps(block - 1, 0, local_steps)
        late = run_block(block, block, late, last=block == n_time - 1, upward=block >= UPWARD)

    for k in range(n_time - 1):
        noise_copy(k).wait_send()

    for copy in sends:
        copy.wait_send()
    for away in range(n_time):
        other = lax.rem(me + away, n_time)
        slot = n_time if away == 0 else other
        done = pltpu.make_async_remote_copy(src_ref=out_stage.at[pl.ds(other * local_steps, local_steps)], dst_ref=gathered.at[:, slot],
                                            send_sem=out_send.at[other], recv_sem=out_recv.at[slot],
                                            device_id={"time": partner}, device_id_type=MESH)
        done.wait_send()
        done.wait_recv()
        if away == 0:
            out_ref[:, me] = out_stage[pl.ds(me * local_steps, local_steps)]
        else:
            out_ref[:, other] = gathered[:, other]


def solution(mesh):
    n_time = mesh.shape["time"]

    def body(x_init, w_in, w_out, mod_scale, mod_shift, step_size, noise_inc):
        local_steps, batch, tokens, channels = noise_inc.shape
        hidden = w_in.shape[1]
        assert batch == n_time and n_time % 2 == 0
        x_t = jnp.swapaxes(x_init, 1, 2)
        noise_t = jnp.swapaxes(noise_inc, 2, 3)
        n_steps = n_time * local_steps
        vmem = pl.BlockSpec(memory_space=pltpu.VMEM)
        anywhere = pl.BlockSpec(memory_space=pl.ANY)
        dma = pltpu.SemaphoreType.DMA
        out = pl.pallas_call(
            functools.partial(sampler_kernel, n_time),
            out_shape=pltpu.VMEM(noise_t.shape, F32),
            in_specs=[anywhere] * 7,
            out_specs=vmem,
            scratch_shapes=[
                pltpu.VMEM((channels, tokens), F32),
                pltpu.VMEM((channels, hidden), BF16),
                pltpu.VMEM((channels, hidden), BF16),
                pltpu.VMEM((local_steps, hidden), BF16),
                pltpu.VMEM((local_steps, hidden), BF16),
                pltpu.SMEM((local_steps,), F32),
                pltpu.VMEM((local_steps, n_time, channels, tokens), F32),
                pltpu.VMEM((hidden, channels), BF16),
                pltpu.VMEM((2 * local_steps, hidden), BF16),
                pltpu.VMEM((2 * local_steps, LANES), F32),
                pltpu.VMEM((n_time, 2 * local_steps, hidden), BF16),
                pltpu.VMEM((n_time, 2 * local_steps, LANES), F32),
                pltpu.VMEM((n_steps, hidden, LANES), F32),
                pltpu.VMEM((n_steps, hidden, LANES), F32),
                pltpu.VMEM((hidden, tokens), F32),
                pltpu.VMEM((n_steps, channels, tokens), F32),
                pltpu.VMEM((2, SWEEPS + 1, channels, tokens), F32),
                pltpu.VMEM((2 * SWEEPS, hidden, tokens), F32),
                pltpu.VMEM((hidden, tokens), F32),
                pltpu.VMEM((hidden, tokens), F32),
                pltpu.VMEM((2 * local_steps, hidden, tokens), F32),
                pltpu.VMEM((n_steps, channels, tokens), F32),
                pltpu.VMEM((n_steps, channels, tokens), F32),
                pltpu.VMEM((local_steps, n_time + 1, channels, tokens), F32),
                dma((7,)), dma((n_time,)), dma((n_time,)), dma((n_time,)), dma((n_time,)),
                dma((n_time,)), dma((n_time,)), dma((n_time,)), dma((n_time + 1,)),
            ],
            compiler_params=pltpu.CompilerParams(collective_id=0, has_side_effects=True),
        )(x_t, w_in, w_out.T, mod_scale, mod_shift, step_size, noise_t)
        return jnp.swapaxes(out, 2, 3)

    return jax.shard_map(
        body,
        mesh=mesh,
        in_specs=(P("data"), P(), P(), P("time"), P("time"), P("time"), P("time", "data")),
        out_specs=P("time", "data"),
        check_vma=False,
    )
```

time: 43 us -> 41.6 us (0.967); the launches traced: 42.9 us -> 40.9 us
  Pallas kernels: 42.1 us -> 40.1 us
    pallas_call x1, Pallas kernels: 42.1 us -> 40.1 us  [body(): pl.pallas_call(functools.partial(sampler_kernel, n_time), out_shape=pltpu...]
where the time goes in v2:
time: 41.6 us; the launch traced here: 40.9 us
  Pallas kernels  40.1 us (96%)
  local copies, waits for them, and re-layouts  0.8 us (2%)
    pallas_call x1, Pallas kernels, body(): pl.pallas_call(functools.partial(sampler_kernel, n_time), out_shape=pltpu...  40.1 us

profile of v2, /device:TPU:119, one launch (start us, length us, event | category | flops | bytes accessed | tf_op | source)
XLA Modules:
  0.0 40.9 jit_solution(4867012760810466693)
XLA Ops:
  0.0 40.1 %shard_map.73 = f32[4,8,16,256]{3,2,1,0:T(8,128)S(1)} custom-call(f32[8,16,256]{2,1,0:T(8,128)} %bitcast.6, bf16[16,384]{1,0:T(8,128)(2,1)} %w_in_ref.1, bf16[16,384]{1,0:T(8,128)(2,1)} %bitcast.7, bf16[4,384]{1,0:T(4,128)(2,1)} %scale_ref.1, bf16[4,384]{1,0:T(4,128)(2,1)} %shift_ref.1, f32[4]{0:T(128)} %step_ref.1, f32[4,8,16,256]{3,2,1,0:T(8,128)} %bitcast.5), custom_call_target="tpu_custom_call" | custom-call | tf_op jit(solution)/shard_map/pallas_call | solution.py:360
  40.1 0.8 %copy.9 = f32[4,8,256,16]{2,3,1,0:T(8,128)} copy(f32[4,8,256,16]{2,3,1,0:T(8,128)S(1)} %bitcast.4) | data formatting | bytes 1048576

commit v3 on v2

--- a/solution.py
+++ b/solution.py
@@ -9,7 +9,6 @@
 from jax.sharding import PartitionSpec as P
 
 SWEEPS = 8
-UPWARD = 6
 LANES = 128
 F32 = jnp.float32
 BF16 = jnp.bfloat16
@@ -157,7 +156,7 @@
     for k in range(local_steps):
         start_tile([other], k)
 
-    @pl.when(me == 1)
+    @pl.when((me >= 1) & (me < 4))
     def _():
         send_noise()
 
@@ -169,7 +168,7 @@
         for k in range(2 * local_steps):
             start_tile(pair, k)
 
-    @pl.when(me >= 2)
+    @pl.when(me >= 4)
     def _():
         send_noise()
 
@@ -185,10 +184,8 @@
         half = pre * wide(mul_all[at]) + wide(add_all[at])
         dst[index] = gelu_of_half(half)
 
-    def first_product(parity, s, parts=1):
-        size = hidden // parts
-        latent = versions[parity, s].astype(BF16)
-        return jnp.concatenate([jnp.dot(w_in_t[k * size:(k + 1) * size, :], latent, preferred_element_type=F32) for k in range(parts)], axis=0)
+    def first_product(parity, s):
+        return jnp.dot(w_in_t[...], versions[parity, s].astype(BF16), preferred_element_type=F32)
 
     def update(block, i, s, act, base=None):
         at = block * local_steps + i
@@ -202,9 +199,8 @@
             if isinstance(block, int):
                 send_ready(block, i + 1)
 
-    def run_block(block, static_block=None, late=(), last=False, filler=(), upward=False):
+    def run_block(block, static_block=None, late=(), last=False, filler=()):
         filler = list(filler)
-        block_parts = last or static_block == 0
         late_act = late_pre = None
         if late:
             late_act, late_pre = late
@@ -225,12 +221,10 @@
             return max(1, low), min(j, SWEEPS - 1), low <= 0
 
         tiles = [(i, s) for i in range(local_steps) for s in range(ranges(i)[1], ranges(i)[0] - 1, -1)]
-        if upward:
-            tiles.sort()
         begun = {}
 
         def begin(tile):
-            begun[tile] = first_product(tile[0] % 2, tile[1], 2 if block_parts else 1)
+            begun[tile] = first_product(tile[0] % 2, tile[1])
 
         pending = []
         for i in range(local_steps):
@@ -243,8 +237,6 @@
                 activate(pre_late[...], late_pre[0] * local_steps + late_pre[1], act_late, ...)
                 pending.append("late")
                 late_act = None
-                if upward:
-                    finish(pending.pop())
             for k, tile in enumerate(mine):
                 if k + 1 < len(mine):
                     begin(mine[k + 1])
@@ -323,7 +315,7 @@
         wait_noise(block)
         if block == full_to:
             send_steps(block - 1, 0, local_steps)
-        late = run_block(block, block, late, last=block == n_time - 1, upward=block >= UPWARD)
+        late = run_block(block, block, late, last=block == n_time - 1)
 
     for k in range(n_time - 1):
         noise_copy(k).wait_send()

time: 41.6 us -> 40.2 us (0.966); the launches traced: 40.9 us -> 40.1 us
  Pallas kernels: 40.1 us -> 39.3 us
    pallas_call x1, Pallas kernels: 40.1 us -> 39.3 us  [body(): pl.pallas_call(functools.partial(sampler_kernel, n_time), out_shape=pltpu...]
where the time goes in v3:
time: 40.2 us; the launch traced here: 40.1 us
  Pallas kernels  39.3 us (98%)
  local copies, waits for them, and re-layouts  0.8 us (2%)
    pallas_call x1, Pallas kernels, body(): pl.pallas_call(functools.partial(sampler_kernel, n_time), out_shape=pltpu...  39.3 us

profile of v3, /device:TPU:119, one launch (start us, length us, event | category | flops | bytes accessed | tf_op | source)
XLA Modules:
  0.0 40.1 jit_solution(70378545684256238)
XLA Ops:
  0.0 39.3 %shard_map.73 = f32[4,8,16,256]{3,2,1,0:T(8,128)S(1)} custom-call(f32[8,16,256]{2,1,0:T(8,128)} %bitcast.6, bf16[16,384]{1,0:T(8,128)(2,1)} %w_in_ref.1, bf16[16,384]{1,0:T(8,128)(2,1)} %bitcast.7, bf16[4,384]{1,0:T(4,128)(2,1)} %scale_ref.1, bf16[4,384]{1,0:T(4,128)(2,1)} %shift_ref.1, f32[4]{0:T(128)} %step_ref.1, f32[4,8,16,256]{3,2,1,0:T(8,128)} %bitcast.5), custom_call_target="tpu_custom_call" | custom-call | tf_op jit(solution)/shard_map/pallas_call | solution.py:352
  39.3 0.8 %copy.9 = f32[4,8,256,16]{2,3,1,0:T(8,128)} copy(f32[4,8,256,16]{2,3,1,0:T(8,128)S(1)} %bitcast.4) | data formatting | bytes 1048576

commit v4 on v3

--- a/solution.py
+++ b/solution.py
@@ -46,11 +46,13 @@
     ]
     for copy in loads:
         copy.start()
-    own_noise = pltpu.make_async_copy(noise_ref.at[:, me], noise_all.at[pl.ds(me * local_steps, local_steps)], noise_recv.at[me])
-    own_noise.start()
+    half_steps = local_steps // 2
+    for part in range(2):
+        pltpu.make_async_copy(noise_ref.at[pl.ds(part * half_steps, half_steps), me],
+                              noise_all.at[pl.ds(me * local_steps + part * half_steps, half_steps)], noise_recv.at[part, me]).start()
     noise_load = pltpu.make_async_copy(noise_ref, noise_buf, load_sem.at[len(loads)])
     noise_load.start()
-    for copy in loads:
+    for copy in loads[:3]:
         copy.wait()
     mod_own[0:local_steps, :] = scale_buf[...]
     mod_own[local_steps:2 * local_steps, :] = shift_buf[...]
@@ -58,14 +60,6 @@
         step_own[i:i + 1, :] = jnp.full((1, LANES), step_buf[i], F32)
     mod_all[me] = mod_own[...]
     step_all[me] = step_own[...]
-    w_in_t[...] = w_in_buf[...].astype(F32).T.astype(BF16)
-
-    x0 = x_buf[...]
-    versions[0, 0] = x0
-    versions[1, 0] = x0
-    out_stage[0] = x0
-    pre_init[...] = jnp.dot(w_in_t[...], x0.astype(BF16), preferred_element_type=F32)
-
     pl.semaphore_wait(barrier, n_time - 1)
 
     sends = []
@@ -85,14 +79,16 @@
         sends.append(send(step_own, step_all.at[me], step_send.at[k], step_recv.at[me], target))
     noise_load.wait()
 
-    def noise_copy(k):
+    def noise_copy(part, k):
         return pltpu.make_async_remote_copy(
-            src_ref=noise_buf.at[:, peers[k]], dst_ref=noise_all.at[pl.ds(me * local_steps, local_steps)],
-            send_sem=noise_send.at[k], recv_sem=noise_recv.at[me], device_id={"time": peers[k]}, device_id_type=MESH)
+            src_ref=noise_buf.at[pl.ds(part * half_steps, half_steps), peers[k]],
+            dst_ref=noise_all.at[pl.ds(me * local_steps + part * half_steps, half_steps)],
+            send_sem=noise_send.at[part, k], recv_sem=noise_recv.at[part, me], device_id={"time": peers[k]}, device_id_type=MESH)
 
     def send_noise():
-        for k in range(n_time - 1):
-            noise_copy(k).start()
+        for part in range(2):
+            for k in range(n_time - 1):
+                noise_copy(part, k).start()
 
     def wait_mods(source):
         pltpu.make_async_copy(mod_own, mod_all.at[source], mod_recv.at[source]).wait()
@@ -143,6 +139,16 @@
     @pl.when(me == 0)
     def _():
         send_noise()
+
+    for copy in loads[3:]:
+        copy.wait()
+    w_in_t[...] = w_in_buf[...].astype(F32).T.astype(BF16)
+
+    x0 = x_buf[...]
+    versions[0, 0] = x0
+    versions[1, 0] = x0
+    out_stage[0] = x0
+    pre_init[...] = jnp.dot(w_in_t[...], x0.astype(BF16), preferred_element_type=F32)
 
     @pl.when(one != me)
     def _():
@@ -229,6 +235,8 @@
         pending = []
         for i in range(local_steps):
             low, high, needs_first = ranges(i)
+            if static_block == 0 and i == half_steps:
+                wait_noise(block, (1,))
             mine = [t for t in tiles if t[0] == i]
             if mine:
                 begin(mine[0])
@@ -269,9 +277,11 @@
         if not last:
             return late_act_out, late_pre_out
 
-    def wait_noise(block):
-        dst = noise_all.at[pl.ds(block * local_steps, local_steps)]
-        pltpu.make_async_copy(noise_ref.at[:, me], dst, noise_recv.at[block]).wait()
+    def wait_noise(block, parts=(0, 1)):
+        for part in parts:
+            pltpu.make_async_copy(noise_ref.at[pl.ds(part * half_steps, half_steps), me],
+                                  noise_all.at[pl.ds(block * local_steps + part * half_steps, half_steps)],
+                                  noise_recv.at[part, block]).wait()
 
     def send_steps(block, first, count):
         own = block == me
@@ -294,7 +304,7 @@
 
     late = ()
     for block in range(full_from):
-        wait_noise(block)
+        wait_noise(block, (0, 1) if block else (0,))
         if block > 0:
             send_steps(block - 1, 0, local_steps)
         filler = [functools.partial(start_tile, pair, k) for k in range(2 * local_steps)] if block == 0 else ()
@@ -317,8 +327,9 @@
             send_steps(block - 1, 0, local_steps)
         late = run_block(block, block, late, last=block == n_time - 1)
 
-    for k in range(n_time - 1):
-        noise_copy(k).wait_send()
+    for part in range(2):
+        for k in range(n_time - 1):
+            noise_copy(part, k).wait_send()
 
     for copy in sends:
         copy.wait_send()
@@ -380,7 +391,7 @@
                 pltpu.VMEM((n_steps, channels, tokens), F32),
                 pltpu.VMEM((local_steps, n_time + 1, channels, tokens), F32),
                 dma((7,)), dma((n_time,)), dma((n_time,)), dma((n_time,)), dma((n_time,)),
-                dma((n_time,)), dma((n_time,)), dma((n_time,)), dma((n_time + 1,)),
+                dma((2, n_time)), dma((2, n_time)), dma((n_time,)), dma((n_time + 1,)),
             ],
             compiler_params=pltpu.CompilerParams(collective_id=0, has_side_effects=True),
         )(x_t, w_in, w_out.T, mod_scale, mod_shift, step_size, noise_t)

time: 40.2 us -> 40 us (level)
  no operation moved by 1% of the time
where the time goes in v4:
time: 40 us; the launch traced here: 39.9 us
  Pallas kernels  39.1 us (98%)
  local copies, waits for them, and re-layouts  0.8 us (2%)
    pallas_call x1, Pallas kernels, body(): pl.pallas_call(functools.partial(sampler_kernel, n_time), out_shape=pltpu...  39.1 us

profile of v4, /device:TPU:119, one launch (start us, length us, event | category | flops | bytes accessed | tf_op | source)
XLA Modules:
  0.0 39.9 jit_solution(12597662915560496010)
XLA Ops:
  0.0 39.1 %shard_map.73 = f32[4,8,16,256]{3,2,1,0:T(8,128)S(1)} custom-call(f32[8,16,256]{2,1,0:T(8,128)} %bitcast.6, bf16[16,384]{1,0:T(8,128)(2,1)} %w_in_ref.1, bf16[16,384]{1,0:T(8,128)(2,1)} %bitcast.7, bf16[4,384]{1,0:T(4,128)(2,1)} %scale_ref.1, bf16[4,384]{1,0:T(4,128)(2,1)} %shift_ref.1, f32[4]{0:T(128)} %step_ref.1, f32[4,8,16,256]{3,2,1,0:T(8,128)} %bitcast.5), custom_call_target="tpu_custom_call" | custom-call | tf_op jit(solution)/shard_map/pallas_call | solution.py:363
  39.1 0.8 %copy.9 = f32[4,8,256,16]{2,3,1,0:T(8,128)} copy(f32[4,8,256,16]{2,3,1,0:T(8,128)S(1)} %bitcast.4) | data formatting | bytes 1048576
